TPU v7x, 32 devices: a whole 2x2x4 slice. The times are simulated.
32 devices in a mesh: blk: 4 (over y, x), grp: 8 (over z, core).
Axes of the slice: x: 2, y: 2, z: 4, core: 2. Of those that a mesh axis runs over, the one named last changes fastest.
Arguments:
- queries: bfloat16 [32, 32, 128], P('blk', 'grp'), may hold values from -3 to 3
- token_counts: int32 [32], P('blk'), may hold values from 8 to 32
- pages: bfloat16 [32, 1024, 128], P(('blk', 'grp')), may hold values from -6 to 6
- patch_counts: int32 [32], P(('blk', 'grp')), may hold values from 512 to 1024
- labels: int32 [32, 32], P(None, ('blk', 'grp')), may hold values 0 or 1
Outputs:
- query_grad: float32 [32, 32, 128], P('blk', 'grp')
- page_grad: float32 [32, 1024, 128], P(('blk', 'grp'))
- page_loss: float32 [32], P(('blk', 'grp'))
All inputs are finite; a program needn't handle non-finite values. No bound on the sum of `labels` on one device may be relied on, other than what follows from the above.
Results may differ from a plain program's by a relative error of at most 0.018.
Values may be sent and summed in bfloat16 or wider, within the bound.
A program may use at most 64 MiB of HBM per device.

v0:
```python
import jax
import jax.numpy as jnp
from jax import lax
from jax.sharding import PartitionSpec as P

align_sharpness = 4.0
logit_scale = 2.0
logit_bias = -5.0


def align(query_rows, counts, page_rows, patch_count, label_column):
    query_number = counts.shape[0]
    token_slots = query_rows.shape[0] // query_number
    scores = jnp.dot(query_rows, page_rows.T, preferred_element_type=jnp.float32)
    patch_mask = jnp.arange(page_rows.shape[0]) < patch_count
    logits = jnp.where(patch_mask[None, :], align_sharpness * scores, -jnp.inf)
    row_max = jnp.max(logits, axis=1, keepdims=True)
    exponent = jnp.exp(logits - row_max)
    weights = exponent / jnp.sum(exponent, axis=1, keepdims=True)
    token_score = jnp.sum(weights * scores, axis=1)
    token_mask = jnp.arange(token_slots)[None, :] < counts[:, None]
    count_float = counts.astype(jnp.float32)
    pair_score = (
        jnp.sum(
            jnp.where(token_mask, token_score.reshape(query_number, token_slots), jnp.float32(0.0)),
            axis=1,
        )
        / count_float
    )
    label_sign = 2.0 * label_column.astype(jnp.float32) - 1.0
    pair_logit = logit_scale * pair_score + logit_bias
    loss_sum = jnp.sum(jax.nn.softplus(-label_sign * pair_logit))
    score_grad = -label_sign * logit_scale * jax.nn.sigmoid(-label_sign * pair_logit)
    token_grad = jnp.where(
        token_mask, (score_grad / count_float)[:, None], jnp.float32(0.0)
    ).reshape(-1)
    scores_grad = (
        token_grad[:, None] * weights * (1.0 + align_sharpness * (scores - token_score[:, None]))
    ).astype(jnp.bfloat16)
    query_term = jnp.dot(scores_grad, page_rows, preferred_element_type=jnp.float32)
    page_term = jnp.dot(scores_grad.T, query_rows, preferred_element_type=jnp.float32)
    return (query_term, page_term, loss_sum)


def local(queries, token_counts, pages, patch_counts, labels):
    page_rows = pages[0]
    patch_count = patch_counts[0]
    label_column = labels[:, 0]
    feature_width = page_rows.shape[1]
    blocks = lax.axis_size("blk")
    groups = lax.axis_size("grp")
    block_queries = token_counts.shape[0]
    gathered = lax.all_gather(queries, "grp", axis=1, tiled=True)
    query_tokens = gathered.shape[1]
    total_queries = block_queries * blocks
    empty_page = jnp.zeros(page_rows.shape, jnp.float32)

    def block_terms(held_queries, held_counts, source):
        labels_here = lax.dynamic_slice_in_dim(label_column, source * block_queries, block_queries)
        return align(
            held_queries.reshape(-1, feature_width),
            held_counts,
            page_rows,
            patch_count,
            labels_here,
        )

    slice_tokens = query_tokens // groups
    buffer = jnp.zeros((blocks * groups * block_queries, slice_tokens, feature_width), jnp.float32)
    piece_queries = lax.all_gather(gathered, "blk", axis=0, tiled=True)
    piece_counts = lax.all_gather(token_counts, "blk", axis=0, tiled=True)
    count_blocks = piece_queries.shape[0] // block_queries

    def one_block(inner_index, state_in):
        page_grad, loss_sum, collected = state_in
        held_queries = lax.dynamic_slice_in_dim(
            piece_queries, inner_index * block_queries, block_queries
        )
        held_counts = lax.dynamic_slice_in_dim(
            piece_counts, inner_index * block_queries, block_queries
        )
        query_term, page_term, loss_term = block_terms(held_queries, held_counts, inner_index)
        arranged = query_term.reshape(block_queries, groups, slice_tokens, feature_width)
        arranged = arranged.transpose(1, 0, 2, 3).reshape(
            groups * block_queries, slice_tokens, feature_width
        )
        collected = lax.dynamic_update_slice_in_dim(
            collected, arranged, inner_index * groups * block_queries, 0
        )
        return (page_grad + page_term, loss_sum + loss_term, collected)

    page_grad, loss_sum, buffer = lax.fori_loop(
        0, count_blocks, one_block, (empty_page, jnp.float32(0.0), buffer)
    )
    query_grad = lax.psum_scatter(buffer, ("blk", "grp"), scatter_dimension=0, tiled=True)
    page_loss = (loss_sum / jnp.float32(total_queries)).reshape(1)
    return (query_grad, page_grad[None], page_loss)


def solution(mesh):
    in_specs = (
        P("blk", "grp", None),
        P("blk"),
        P(("blk", "grp"), None, None),
        P(("blk", "grp")),
        P(None, ("blk", "grp")),
    )
    out_specs = (P("blk", "grp", None), P(("blk", "grp"), None, None), P(("blk", "grp")))
    return jax.shard_map(local, mesh=mesh, in_specs=in_specs, out_specs=out_specs, check_vma=False)
```

profile of v0, /device:TPU:0, one launch (start us, length us, event | category | flops | bytes accessed | tf_op | source)
XLA Modules:
  0.0 203.5 jit_solution(7265506860128643885)
XLA Ops:
  7.2 0.7 copy.13
  7.9 15.7 %all_gather.10 = bf16[8,32,128]{2,0,1:T(8,128)(2,1)S(1)} all-gather(bf16[8,4,128]{2,0,1:T(8,128)(2,1)S(1)} %copy.13), channel_id=1, replica_groups=mesh['blk'=4,'grp'=8] {'grp'}, dimensions={1}, use_global_device_ids=true | all-gather | bytes 73728 | tf_op jit(solution)/shard_map/all_gather | solution.py:53
  23.6 9.0 %all_gather.11 = bf16[32,32,128]{2,1,0:T(8,128)(2,1)S(1)} all-gather(bf16[8,32,128]{2,1,0:T(8,128)(2,1)S(1)} %copy.14), channel_id=1, replica_groups=mesh['blk'=4,'grp'=8] {'blk'}, dimensions={0}, use_global_device_ids=true | all-gather | bytes 327680 | tf_op jit(solution)/shard_map/all_gather | solution.py:70
  32.6 0.7 copy-done.5
  33.3 0.6 dynamic-slice
  34.5 0.6 copy-done.4
  35.3 7.3 %all-reduce = s32[32]{0:T(128)S(1)} all-reduce(s32[32]{0:T(128)S(1)} %dynamic-update-slice), channel_id=1, replica_groups=mesh['blk'=4,'grp'=8] {'blk'}, use_global_device_ids=true, to_apply=%add | all-reduce | flops 32 | bytes 256
  42.8 0.9 copy-done
  43.6 20.4 %while.20 = (s32[]{:T(128)}, f32[1024,128]{1,0:T(8,128)S(1)}, f32[]{:T(128)}, f32[256,4,128]{2,1,0:T(4,128)S(1)}, s32[32]{0:T(128)S(1)}, /*index=5*/s32[32]{0:T(...) while((s32[]{:T(128)}, f32[1024,128]{1,0:T(8,128)S(1)}, ...), condition=%wide.region_6.7_spmd.clone, body=%wide.region_0.6_spmd.clone.sunk | while | flops 207619808 | bytes 8279771 | solution.py:92
  43.7 0.7 iota_compare_fusion.3
  45.0 0.4 multiply_reduce_fusion.2
  45.8 0.7 fusion.33
  46.8 0.5 multiply_convert_fusion.2
  47.6 0.5 convolution_add_fusion.2
  48.7 0.7 iota_compare_fusion.3
  50.1 0.4 multiply_reduce_fusion.2
  50.9 0.7 fusion.33
  51.9 0.5 multiply_convert_fusion.2
  52.7 0.5 convolution_add_fusion.2
  53.8 0.7 iota_compare_fusion.3
  55.2 0.4 multiply_reduce_fusion.2
  56.0 0.7 fusion.33
  56.9 0.5 multiply_convert_fusion.2
  57.8 0.5 convolution_add_fusion.2
  58.9 0.7 iota_compare_fusion.3
  60.3 0.4 multiply_reduce_fusion.2
  61.1 0.7 fusion.33
  62.0 0.5 multiply_convert_fusion.2
  62.9 0.5 convolution_add_fusion.2
  64.0 0.8 copy-done.2
  64.8 129.3 %all-reduce.4.cloned.1.call-done = f32[256,4,128]{2,1,0:T(4,128)} async-done(((f32[256,4,128]{2,1,0:T(4,128)}), f32[256,4,128]{2,1,0:T(4,128)}) %all-reduce.4.cloned.1.call-update) | async-done | bytes 524304
  194.1 1.3 constant_dynamic-slice_fusion.1
  (63 shorter events, 6.9 us)
Async XLA Ops:
  7.2 187.0 %all-reduce.4.cloned.1.call-start = ((), (), s32[]{:S(2)}) async-start(), calls=%async_computation | async-start | bytes 1048576
  32.6 0.7 copy-start.5
  34.5 0.7 copy-start.4
  42.7 0.9 copy-start
  42.8 0.9 copy-start.3
  64.0 0.8 copy-start.2
  64.0 131.5 %copy-start.1 = (f32[1024,128]{1,0:T(8,128)}, f32[1024,128]{1,0:T(8,128)S(1)}, u32[]{:S(2)}) copy-start(f32[1024,128]{1,0:T(8,128)S(1)} %get-tuple-element.227) | copy-start | bytes 1572868
Sparse Core Ops, SparseCore 0:
  65.0 129.1 all-reduce.3
where the time goes:
time: 204 us; the launch traced here: 203 us
  waiting for transfers between devices  129 us (63%)
  blocking collectives  32 us (16%)
  between operations  15.9 us (8%)
  other arithmetic  11.7 us (6%)
  local copies, waits for them, and re-layouts  6.99 us (3%)
  matrix products  4.52 us (2%)
  loops' own time  2.95 us (1%)
    unnamed x2, waiting for transfers between devices  129 us
    all_gather x1, blocking collectives, local(): gathered = lax.all_gather(queries, 'grp', axis=1, tiled=True)  15.7 us
    all_gather x1, blocking collectives, local(): piece_queries = lax.all_gather(gathered, 'blk', axis=0, tiled=True)  8.99 us
    unnamed x1, blocking collectives  7.34 us
    unnamed x17, local copies, waits for them, and re-layouts  5.76 us
  transfers between devices with their start and end apart: 1, of which 1 were waited for; matrix products, arithmetic and copies ran while one was open for 0% of the time, Pallas kernels for 0%

commit v1 on v0

--- a/solution.py
+++ b/solution.py
@@ -50,7 +50,12 @@
     blocks = lax.axis_size("blk")
     groups = lax.axis_size("grp")
     block_queries = token_counts.shape[0]
-    gathered = lax.all_gather(queries, "grp", axis=1, tiled=True)
+    ring = [queries]
+    for hop in range(7):
+        ring.append(lax.ppermute(ring[-1], "grp", [(dev, (dev + 1) % 8) for dev in range(8)]))
+    gathered = jnp.roll(
+        jnp.concatenate(ring[::-1], axis=1), (lax.axis_index("grp") + 1) * ring[0].shape[1], axis=1
+    )
     query_tokens = gathered.shape[1]
     total_queries = block_queries * blocks
     empty_page = jnp.zeros(page_rows.shape, jnp.float32)

time: 204 us -> 216 us (1.059)
  waiting for transfers between devices: 129 us -> 156 us
  blocking collectives: 32 us -> 16.8 us
    ppermute x0 -> x7, waiting for transfers between devices: none -> 29.9 us  [local(): lax.ppermute(ring[-1], 'grp', [(dev, (dev + 1) % 8) for dev in range(8)])]
    all_gather x1 -> x0, blocking collectives: 15.7 us -> none  [local(): gathered = lax.all_gather(queries, 'grp', axis=1, tiled=True)]
    unnamed x2, waiting for transfers between devices: 129 us -> 127 us
    unnamed x17 -> x18, local copies, waits for them, and re-layouts: 5.76 us -> 5.05 us
  transfers between devices with their start and end apart: 1 -> 8, of which waited for: 1 -> 7; matrix products, arithmetic and copies ran while one was open for 0% -> 0% of each run, Pallas kernels for 0% -> 0%
where the time goes in v1:
time: 216 us
  waiting for transfers between devices  156 us (72%)
  blocking collectives  16.8 us (8%)
  between operations  15.9 us (7%)
  other arithmetic  11.8 us (5%)
  local copies, waits for them, and re-layouts  6.56 us (3%)
  matrix products  4.52 us (2%)
  loops' own time  2.94 us (1%)
    unnamed x2, waiting for transfers between devices  127 us
    ppermute x7, waiting for transfers between devices, local(): lax.ppermute(ring[-1], 'grp', [(dev, (dev + 1) % 8) for dev in range(8)])  29.9 us
    all_gather x1, blocking collectives, local(): piece_queries = lax.all_gather(gathered, 'blk', axis=0, tiled=True)  8.97 us
    unnamed x1, blocking collectives  7.87 us
    unnamed x18, local copies, waits for them, and re-layouts  5.05 us
  transfers between devices with their start and end apart: 8, of which 7 were waited for; matrix products, arithmetic and copies ran while one was open for 0% of the time, Pallas kernels for 0%

profile of v1, /device:TPU:0, one launch (start us, length us, event | category | flops | bytes accessed | tf_op | source)
XLA Modules:
  0.0 215.6 jit_solution(10955283956107538234)
XLA Ops:
  7.2 0.5 collective-permute-start
  7.8 5.6 %collective-permute-done = bf16[8,4,128]{2,1,0:T(4,128)(2,1)S(1)} collective-permute-done((bf16[8,4,128]{2,1,0:T(4,128)(2,1)}, bf16[8,4,128]{2,1,0:T(4,128)(2,1)S(1)}, u32[]{:S(2)}, u32[]{:S(2)}) %collective-permute-start) | collective-permute-done | bytes 8224 | tf_op jit(solution)/shard_map/ppermute | solution.py:55
  13.3 4.9 %collective-permute-done.1 = bf16[8,4,128]{2,1,0:T(4,128)(2,1)S(1)} collective-permute-done((bf16[8,4,128]{2,1,0:T(4,128)(2,1)S(1)}, bf16[8,4,128]{2,1,0:T(4,128)(2,1)S(1)}, u32[]{:S(2)}, u32[]{:S(2)}) %collective-permute-start.1) | collective-permute-done | bytes 8224 | tf_op jit(solution)/shard_map/ppermute | solution.py:55
  18.2 4.9 %collective-permute-done.2 = bf16[8,4,128]{2,1,0:T(4,128)(2,1)S(1)} collective-permute-done((bf16[8,4,128]{2,1,0:T(4,128)(2,1)S(1)}, bf16[8,4,128]{2,1,0:T(4,128)(2,1)S(1)}, u32[]{:S(2)}, u32[]{:S(2)}) %collective-permute-start.2) | collective-permute-done | bytes 8224 | tf_op jit(solution)/shard_map/ppermute | solution.py:55
  23.1 4.9 %collective-permute-done.3 = bf16[8,4,128]{2,1,0:T(4,128)(2,1)S(1)} collective-permute-done((bf16[8,4,128]{2,1,0:T(4,128)(2,1)S(1)}, bf16[8,4,128]{2,1,0:T(4,128)(2,1)S(1)}, u32[]{:S(2)}, u32[]{:S(2)}) %collective-permute-start.3) | collective-permute-done | bytes 8224 | tf_op jit(solution)/shard_map/ppermute | solution.py:55
  28.0 4.9 %collective-permute-done.4 = bf16[8,4,128]{2,1,0:T(4,128)(2,1)S(1)} collective-permute-done((bf16[8,4,128]{2,1,0:T(4,128)(2,1)S(1)}, bf16[8,4,128]{2,1,0:T(4,128)(2,1)S(1)}, u32[]{:S(2)}, u32[]{:S(2)}) %collective-permute-start.4) | collective-permute-done | bytes 8224 | tf_op jit(solution)/shard_map/ppermute | solution.py:55
  32.8 4.9 %collective-permute-done.5 = bf16[8,4,128]{2,1,0:T(4,128)(2,1)S(1)} collective-permute-done((bf16[8,4,128]{2,1,0:T(4,128)(2,1)S(1)}, bf16[8,4,128]{2,1,0:T(4,128)(2,1)S(1)}, u32[]{:S(2)}, u32[]{:S(2)}) %collective-permute-start.5) | collective-permute-done | bytes 8224 | tf_op jit(solution)/shard_map/ppermute | solution.py:55
  37.7 0.6 copy-done.6
  38.4 0.6 dynamic-slice
  39.6 0.6 copy-done.5
  40.4 7.9 %all-reduce = s32[32]{0:T(128)S(1)} all-reduce(s32[32]{0:T(128)S(1)} %dynamic-update-slice), channel_id=1, replica_groups=mesh['blk'=4,'grp'=8] {'blk'}, use_global_device_ids=true, to_apply=%add | all-reduce | flops 32 | bytes 256
  48.6 9.0 %all_gather.7 = bf16[32,32,128]{2,1,0:T(8,128)(2,1)S(1)} all-gather(bf16[8,32,128]{2,1,0:T(8,128)(2,1)S(1)} %constant_dynamic-slice_fusion.2), channel_id=1, replica_groups=mesh['blk'=4,'grp'=8] {'blk'}, dimensions={0}, use_global_device_ids=true | all-gather | bytes 327680 | tf_op jit(solution)/shard_map/all_gather | solution.py:75
  57.7 0.9 copy-done
  58.5 20.4 %while.20 = (s32[]{:T(128)}, f32[1024,128]{1,0:T(8,128)S(1)}, f32[]{:T(128)}, f32[256,4,128]{2,1,0:T(4,128)S(1)}, s32[32]{0:T(128)S(1)}, /*index=5*/s32[32]{0:T(...) while((s32[]{:T(128)}, f32[1024,128]{1,0:T(8,128)S(1)}, ...), condition=%wide.region_6.7_spmd.clone, body=%wide.region_0.6_spmd.clone.sunk | while | flops 207619808 | bytes 8279771 | solution.py:97
  58.5 0.7 iota_compare_fusion.3
  60.7 0.7 fusion.33
  61.6 0.5 multiply_convert_fusion.2
  62.5 0.5 convolution_add_fusion.2
  63.6 0.7 iota_compare_fusion.3
  65.8 0.7 fusion.33
  66.7 0.5 multiply_convert_fusion.2
  67.6 0.5 convolution_add_fusion.2
  68.7 0.7 iota_compare_fusion.3
  70.9 0.7 fusion.33
  72.7 0.5 convolution_add_fusion.2
  73.8 0.7 iota_compare_fusion.3
  76.0 0.7 fusion.33
  76.9 0.5 multiply_convert_fusion.2
  77.8 0.5 convolution_add_fusion.2
  78.9 0.8 copy-done.2
  79.7 126.5 %all-reduce.4.cloned.1.call-done = f32[256,4,128]{2,1,0:T(4,128)} async-done(((f32[256,4,128]{2,1,0:T(4,128)}), f32[256,4,128]{2,1,0:T(4,128)}) %all-reduce.4.cloned.1.call-update) | async-done | bytes 524304
  206.3 1.3 constant_dynamic-slice_fusion.1
  (78 shorter events, 9.4 us)
Async XLA Ops:
  7.2 199.1 %all-reduce.4.cloned.1.call-start = ((), (), s32[]{:S(2)}) async-start(), calls=%async_computation | async-start | bytes 1048576
  7.2 6.1 %collective-permute-start = (bf16[8,4,128]{2,1,0:T(4,128)(2,1)}, bf16[8,4,128]{2,1,0:T(4,128)(2,1)S(1)}, u32[]{:S(2)}, u32[]{:S(2)}) collective-permute-start(bf16[8,4,128]{2,1,0:T(4,128)(2,1)} %param.7), channel_id=1, source_target_pairs={{0,1},{1,2},{2,3},{3,4},{4,5},{5,6},{6,7},{7,0},{8,9},{9,10},{10,1... | collective-permute-start | bytes 24584 | tf_op jit(solution)/shard_map/ppermute | solution.py:55
  13.3 4.9 %collective-permute-start.1 = (bf16[8,4,128]{2,1,0:T(4,128)(2,1)S(1)}, bf16[8,4,128]{2,1,0:T(4,128)(2,1)S(1)}, u32[]{:S(2)}, u32[]{:S(2)}) collective-permute-start(bf16[8,4,128]{2,1,0:T(4,128)(2,1)S(1)} %collective-permute-done), channel_id=1, source_target_pairs={{0,1},{1,2},{2,3},{3,4},{4,5},{5,6},{6,7},{7,0},{8,9},{9,10},{10,1... | collective-permute-start | bytes 24584 | tf_op jit(solution)/shard_map/ppermute | solution.py:55
  18.2 4.9 %collective-permute-start.2 = (bf16[8,4,128]{2,1,0:T(4,128)(2,1)S(1)}, bf16[8,4,128]{2,1,0:T(4,128)(2,1)S(1)}, u32[]{:S(2)}, u32[]{:S(2)}) collective-permute-start(bf16[8,4,128]{2,1,0:T(4,128)(2,1)S(1)} %collective-permute-done.1), channel_id=1, source_target_pairs={{0,1},{1,2},{2,3},{3,4},{4,5},{5,6},{6,7},{7,0},{8,9},{9,10},{10,1... | collective-permute-start | bytes 24584 | tf_op jit(solution)/shard_map/ppermute | solution.py:55
  23.1 4.9 %collective-permute-start.3 = (bf16[8,4,128]{2,1,0:T(4,128)(2,1)S(1)}, bf16[8,4,128]{2,1,0:T(4,128)(2,1)S(1)}, u32[]{:S(2)}, u32[]{:S(2)}) collective-permute-start(bf16[8,4,128]{2,1,0:T(4,128)(2,1)S(1)} %collective-permute-done.2), channel_id=1, source_target_pairs={{0,1},{1,2},{2,3},{3,4},{4,5},{5,6},{6,7},{7,0},{8,9},{9,10},{10,1... | collective-permute-start | bytes 24584 | tf_op jit(solution)/shard_map/ppermute | solution.py:55
  28.0 4.9 %collective-permute-start.4 = (bf16[8,4,128]{2,1,0:T(4,128)(2,1)S(1)}, bf16[8,4,128]{2,1,0:T(4,128)(2,1)S(1)}, u32[]{:S(2)}, u32[]{:S(2)}) collective-permute-start(bf16[8,4,128]{2,1,0:T(4,128)(2,1)S(1)} %collective-permute-done.3), channel_id=1, source_target_pairs={{0,1},{1,2},{2,3},{3,4},{4,5},{5,6},{6,7},{7,0},{8,9},{9,10},{10,1... | collective-permute-start | bytes 24584 | tf_op jit(solution)/shard_map/ppermute | solution.py:55
  32.8 4.9 %collective-permute-start.5 = (bf16[8,4,128]{2,1,0:T(4,128)(2,1)S(1)}, bf16[8,4,128]{2,1,0:T(4,128)(2,1)S(1)}, u32[]{:S(2)}, u32[]{:S(2)}) collective-permute-start(bf16[8,4,128]{2,1,0:T(4,128)(2,1)S(1)} %collective-permute-done.4), channel_id=1, source_target_pairs={{0,1},{1,2},{2,3},{3,4},{4,5},{5,6},{6,7},{7,0},{8,9},{9,10},{10,1... | collective-permute-start | bytes 24584 | tf_op jit(solution)/shard_map/ppermute | solution.py:55
  37.7 10.6 %collective-permute-start.6 = (bf16[8,4,128]{2,1,0:T(4,128)(2,1)S(1)}, bf16[8,4,128]{2,1,0:T(4,128)(2,1)S(1)}, u32[]{:S(2)}, u32[]{:S(2)}) collective-permute-start(bf16[8,4,128]{2,1,0:T(4,128)(2,1)S(1)} %collective-permute-done.5), channel_id=1, source_target_pairs={{0,1},{1,2},{2,3},{3,4},{4,5},{5,6},{6,7},{7,0},{8,9},{9,10},{10,1... | collective-permute-start | bytes 24584 | tf_op jit(solution)/shard_map/ppermute | solution.py:55
  37.7 0.7 copy-start.6
  37.7 10.6 %copy-start.4 = (bf16[8,4,128]{2,1,0:T(4,128)(2,1)S(1)}, bf16[8,4,128]{2,1,0:T(4,128)(2,1)}, u32[]{:S(2)}) copy-start(bf16[8,4,128]{2,1,0:T(4,128)(2,1)} %param.7) | copy-start | bytes 24580
  39.6 0.7 copy-start.5
  57.6 1.0 copy-start
  57.7 0.9 copy-start.3
  78.9 0.8 copy-start.2
  78.9 128.7 %copy-start.1 = (f32[1024,128]{1,0:T(8,128)}, f32[1024,128]{1,0:T(8,128)S(1)}, u32[]{:S(2)}) copy-start(f32[1024,128]{1,0:T(8,128)S(1)} %get-tuple-element.227) | copy-start | bytes 1572868
Sparse Core Ops, SparseCore 0:
  79.9 126.3 all-reduce.3
